TPU v7x, 16 devices: a whole 2x2x2 slice. The times are simulated.
16 devices in a mesh: col: 2 (over z), row: 8 (over y, x, core).
Axes of the slice: x: 2, y: 2, z: 2, core: 2. Of those that a mesh axis runs over, the one named last changes fastest.
Arguments:
- matrix: bfloat16 [16384, 16384], P('row', 'col')
- y_start: float32 [16384, 128], P(('col', 'row'))
- center: float32 [], replicated
- half_width: float32 [], replicated
Outputs:
- output 1: float32 [16384, 128], P(('col', 'row'))
- output 2: float32 [128, 128], replicated
All inputs are finite; a program needn't handle non-finite values.
Results may differ from a plain program's by a relative error of at most 0.0143295.
Values are sent between devices in bfloat16 or wider.
A program may use at most 1 GiB of HBM per device.

v0:
```python
import jax
import jax.numpy as jnp
from jax import lax
from jax.sharding import PartitionSpec as P

DEGREE = 8


def solution(mesh):
    row_count = mesh.shape["row"]
    col_count = mesh.shape["col"]
    both_axes = ("col", "row")
    realign_pairs = [(col_idx * row_count + row_idx, row_idx * col_count + col_idx) for row_idx in range(row_count) for col_idx in range(col_count)]

    def apply_matrix(mat_tile, y_low):
        src_block = lax.all_gather(y_low, "row", axis=0, tiled=True)
        part_sum = jnp.dot(mat_tile, src_block, preferred_element_type=jnp.float32)
        folded = lax.psum_scatter(part_sum, "col", scatter_dimension=0, tiled=True)
        return lax.ppermute(folded, both_axes, realign_pairs)

    def local_filter(mat_tile, y_start, center, half_width):
        y_prev = y_start
        y_cur = (apply_matrix(mat_tile, y_start.astype(jnp.bfloat16)) - center * y_start) / half_width
        for step_index in range(DEGREE - 1):
            y_next = 2.0 * (apply_matrix(mat_tile, y_cur.astype(jnp.bfloat16)) - center * y_cur) / half_width - y_prev
            y_prev = y_cur
            y_cur = y_next
        y_low = y_cur.astype(jnp.bfloat16)
        image_low = apply_matrix(mat_tile, y_low).astype(jnp.bfloat16)
        local_gram = jnp.einsum("pa,pb->ab", y_low, image_low, preferred_element_type=jnp.float32)
        gram_mat = lax.psum(local_gram, both_axes) / (mat_tile.shape[0] * row_count)
        return y_cur, gram_mat

    return jax.shard_map(local_filter, mesh=mesh, in_specs=(P("row", "col"), P(both_axes, None), P(), P()), out_specs=(P(both_axes, None), P()), check_vma=False)
```

profile of v0, /device:TPU:0, one launch (start us, length us, event | category | flops | bytes accessed | tf_op | source)
XLA Modules:
  0.0 728.3 jit_solution(5421227816541477615)
XLA Ops:
  7.2 1.8 convert_element_type.30
  9.1 27.9 %all-gather.10.cloned.1.call-done = bf16[8192,128]{1,0:T(8,128)(2,1)} async-done(((bf16[1024,128]{1,0:T(8,128)(2,1)}), bf16[8192,128]{1,0:T(8,128)(2,1)}) %all-gather.10.cloned.1.call-update) | async-done | bytes 2097168 | tf_op jit(solution)/shard_map/all_gather | solution.py:16
  37.0 16.4 %fusion.10 = f32[2048,128]{1,0:T(8,128)} fusion(bf16[2048,8192]{1,0:T(8,128)(2,1)} %param.4, bf16[8192,128]{1,0:T(8,128)(2,1)} %all-gather.10.cloned.1.call-done), kind=kOutput, calls=%fused_computation.27 | convolution fusion | flops 4294967296 | bytes 36700160 | tf_op jit(solution)/shard_map/dot_general | solution.py:17
  53.5 18.5 %reduce-scatter.10.cloned.1.call-done = f32[1024,128]{1,0:T(8,128)} async-done(((f32[2048,128]{1,0:T(8,128)}), f32[1024,128]{1,0:T(8,128)}) %reduce-scatter.10.cloned.1.call-update) | async-done | bytes 524304 | tf_op jit(solution)/shard_map/reduce_scatter | solution.py:18
  72.0 1.7 collective-permute-start
  75.9 32.2 %all-gather.12.cloned.1.call-done = bf16[8192,128]{1,0:T(8,128)(2,1)} async-done(((bf16[1024,128]{1,0:T(8,128)(2,1)}), bf16[8192,128]{1,0:T(8,128)(2,1)}) %all-gather.12.cloned.1.call-update) | async-done | bytes 2097168 | tf_op jit(solution)/shard_map/all_gather | solution.py:16
  108.2 16.4 %convolution_bitcast_fusion.6 = f32[2048,128]{1,0:T(8,128)} fusion(bf16[2048,8192]{1,0:T(8,128)(2,1)} %param.4, bf16[8192,128]{1,0:T(8,128)(2,1)} %all-gather.12.cloned.1.call-done), kind=kOutput, calls=%fused_computation.6 | convolution fusion | flops 4294967296 | bytes 36700160 | tf_op jit(solution)/shard_map/dot_general | solution.py:17
  124.7 18.5 %reduce-scatter.12.cloned.1.call-done = f32[1024,128]{1,0:T(8,128)} async-done(((f32[2048,128]{1,0:T(8,128)}), f32[1024,128]{1,0:T(8,128)}) %reduce-scatter.12.cloned.1.call-update) | async-done | bytes 524304 | tf_op jit(solution)/shard_map/reduce_scatter | solution.py:18
  143.2 1.7 collective-permute-start.1
  145.8 33.6 %all-gather.14.cloned.1.call-done = bf16[8192,128]{1,0:T(8,128)(2,1)} async-done(((bf16[1024,128]{1,0:T(8,128)(2,1)}), bf16[8192,128]{1,0:T(8,128)(2,1)}) %all-gather.14.cloned.1.call-update) | async-done | bytes 2097168 | tf_op jit(solution)/shard_map/all_gather | solution.py:16
  179.4 16.4 %convolution_bitcast_fusion.5 = f32[2048,128]{1,0:T(8,128)} fusion(bf16[2048,8192]{1,0:T(8,128)(2,1)} %param.4, bf16[8192,128]{1,0:T(8,128)(2,1)} %all-gather.14.cloned.1.call-done), kind=kOutput, calls=%fused_computation.5 | convolution fusion | flops 4294967296 | bytes 36700160 | tf_op jit(solution)/shard_map/dot_general | solution.py:17
  195.9 18.5 %reduce-scatter.14.cloned.1.call-done = f32[1024,128]{1,0:T(8,128)} async-done(((f32[2048,128]{1,0:T(8,128)}), f32[1024,128]{1,0:T(8,128)}) %reduce-scatter.14.cloned.1.call-update) | async-done | bytes 524304 | tf_op jit(solution)/shard_map/reduce_scatter | solution.py:18
  214.4 1.7 collective-permute-start.2
  217.3 33.4 %all-gather.16.cloned.1.call-done = bf16[8192,128]{1,0:T(8,128)(2,1)} async-done(((bf16[1024,128]{1,0:T(8,128)(2,1)}), bf16[8192,128]{1,0:T(8,128)(2,1)}) %all-gather.16.cloned.1.call-update) | async-done | bytes 2097168 | tf_op jit(solution)/shard_map/all_gather | solution.py:16
  250.6 16.4 %convolution_bitcast_fusion.4 = f32[2048,128]{1,0:T(8,128)} fusion(bf16[2048,8192]{1,0:T(8,128)(2,1)} %param.4, bf16[8192,128]{1,0:T(8,128)(2,1)} %all-gather.16.cloned.1.call-done), kind=kOutput, calls=%fused_computation.4 | convolution fusion | flops 4294967296 | bytes 36700160 | tf_op jit(solution)/shard_map/dot_general | solution.py:17
  267.1 18.5 %reduce-scatter.16.cloned.1.call-done = f32[1024,128]{1,0:T(8,128)} async-done(((f32[2048,128]{1,0:T(8,128)}), f32[1024,128]{1,0:T(8,128)}) %reduce-scatter.16.cloned.1.call-update) | async-done | bytes 524304 | tf_op jit(solution)/shard_map/reduce_scatter | solution.py:18
  288.3 33.6 %all-gather.18.cloned.1.call-done = bf16[8192,128]{1,0:T(8,128)(2,1)} async-done(((bf16[1024,128]{1,0:T(8,128)(2,1)}), bf16[8192,128]{1,0:T(8,128)(2,1)}) %all-gather.18.cloned.1.call-update) | async-done | bytes 2097168 | tf_op jit(solution)/shard_map/all_gather | solution.py:16
  321.8 16.4 %convolution_bitcast_fusion.3 = f32[2048,128]{1,0:T(8,128)} fusion(bf16[2048,8192]{1,0:T(8,128)(2,1)} %param.4, bf16[8192,128]{1,0:T(8,128)(2,1)} %all-gather.18.cloned.1.call-done), kind=kOutput, calls=%fused_computation.3 | convolution fusion | flops 4294967296 | bytes 36700160 | tf_op jit(solution)/shard_map/dot_general | solution.py:17
  338.3 18.5 %reduce-scatter.18.cloned.1.call-done = f32[1024,128]{1,0:T(8,128)} async-done(((f32[2048,128]{1,0:T(8,128)}), f32[1024,128]{1,0:T(8,128)}) %reduce-scatter.18.cloned.1.call-update) | async-done | bytes 524304 | tf_op jit(solution)/shard_map/reduce_scatter | solution.py:18
  359.4 33.6 %all-gather.20.cloned.1.call-done = bf16[8192,128]{1,0:T(8,128)(2,1)} async-done(((bf16[1024,128]{1,0:T(8,128)(2,1)}), bf16[8192,128]{1,0:T(8,128)(2,1)}) %all-gather.20.cloned.1.call-update) | async-done | bytes 2097168 | tf_op jit(solution)/shard_map/all_gather | solution.py:16
  393.0 16.4 %convolution_bitcast_fusion.2 = f32[2048,128]{1,0:T(8,128)} fusion(bf16[2048,8192]{1,0:T(8,128)(2,1)} %param.4, bf16[8192,128]{1,0:T(8,128)(2,1)} %all-gather.20.cloned.1.call-done), kind=kOutput, calls=%fused_computation.2 | convolution fusion | flops 4294967296 | bytes 36700160 | tf_op jit(solution)/shard_map/dot_general | solution.py:17
  409.5 18.5 %reduce-scatter.20.cloned.1.call-done = f32[1024,128]{1,0:T(8,128)} async-done(((f32[2048,128]{1,0:T(8,128)}), f32[1024,128]{1,0:T(8,128)}) %reduce-scatter.20.cloned.1.call-update) | async-done | bytes 524304 | tf_op jit(solution)/shard_map/reduce_scatter | solution.py:18
  430.8 33.3 %all-gather.22.cloned.1.call-done = bf16[8192,128]{1,0:T(8,128)(2,1)} async-done(((bf16[1024,128]{1,0:T(8,128)(2,1)}), bf16[8192,128]{1,0:T(8,128)(2,1)}) %all-gather.22.cloned.1.call-update) | async-done | bytes 2097168 | tf_op jit(solution)/shard_map/all_gather | solution.py:16
  464.2 16.4 %convolution_bitcast_fusion.1 = f32[2048,128]{1,0:T(8,128)} fusion(bf16[2048,8192]{1,0:T(8,128)(2,1)} %param.4, bf16[8192,128]{1,0:T(8,128)(2,1)} %all-gather.22.cloned.1.call-done), kind=kOutput, calls=%fused_computation.1 | convolution fusion | flops 4294967296 | bytes 36700160 | tf_op jit(solution)/shard_map/dot_general | solution.py:17
  480.7 18.5 %reduce-scatter.22.cloned.1.call-done = f32[1024,128]{1,0:T(8,128)} async-done(((f32[2048,128]{1,0:T(8,128)}), f32[1024,128]{1,0:T(8,128)}) %reduce-scatter.22.cloned.1.call-update) | async-done | bytes 524304 | tf_op jit(solution)/shard_map/reduce_scatter | solution.py:18
  501.8 33.6 %all-gather.24.cloned.1.call-done = bf16[8192,128]{1,0:T(8,128)(2,1)} async-done(((bf16[1024,128]{1,0:T(8,128)(2,1)}), bf16[8192,128]{1,0:T(8,128)(2,1)}) %all-gather.24.cloned.1.call-update) | async-done | bytes 2097168 | tf_op jit(solution)/shard_map/all_gather | solution.py:16
  535.3 16.4 %convolution_bitcast_fusion = f32[2048,128]{1,0:T(8,128)} fusion(bf16[2048,8192]{1,0:T(8,128)(2,1)} %param.4, bf16[8192,128]{1,0:T(8,128)(2,1)} %all-gather.24.cloned.1.call-done), kind=kOutput, calls=%fused_computation | convolution fusion | flops 4294967296 | bytes 36700160 | tf_op jit(solution)/shard_map/dot_general | solution.py:17
  551.9 18.5 %reduce-scatter.24.cloned.1.call-done = f32[1024,128]{1,0:T(8,128)} async-done(((f32[2048,128]{1,0:T(8,128)}), f32[1024,128]{1,0:T(8,128)}) %reduce-scatter.24.cloned.1.call-update) | async-done | bytes 524304 | tf_op jit(solution)/shard_map/reduce_scatter | solution.py:18
  573.3 33.6 %all-gather.26.cloned.1.call-done = bf16[8192,128]{1,0:T(8,128)(2,1)} async-done(((bf16[1024,128]{1,0:T(8,128)(2,1)}), bf16[8192,128]{1,0:T(8,128)(2,1)}) %all-gather.26.cloned.1.call-update) | async-done | bytes 2097168 | tf_op jit(solution)/shard_map/all_gather | solution.py:16
  606.8 17.5 %convolution_bitcast_fusion.7 = f32[2048,128]{0,1:T(8,128)} fusion(bf16[8192,128]{1,0:T(8,128)(2,1)} %all-gather.26.cloned.1.call-done, bf16[2048,8192]{1,0:T(8,128)(2,1)} %param.4), kind=kOutput, calls=%fused_computation.7 | convolution fusion | flops 4294967296 | bytes 36700160 | tf_op jit(solution)/shard_map/dot_general | solution.py:17
  624.4 18.5 %reduce-scatter.26.cloned.1.call-done = f32[1024,128]{0,1:T(8,128)} async-done(((f32[2048,128]{0,1:T(8,128)}), f32[1024,128]{0,1:T(8,128)}) %reduce-scatter.26.cloned.1.call-update) | async-done | bytes 524304 | tf_op jit(solution)/shard_map/reduce_scatter | solution.py:18
  645.5 74.8 %all-reduce.2.cloned.1.call-done = f32[128,128]{1,0:T(8,128)} async-done(((f32[128,128]{1,0:T(8,128)}), f32[128,128]{1,0:T(8,128)}) %all-reduce.2.cloned.1.call-update) | async-done | bytes 65552 | tf_op jit(solution)/shard_map/psum | solution.py:31
  (67 shorter events, 20.9 us)
Async XLA Ops:
  7.2 29.8 %all-gather.10.cloned.1.call-start = ((), (), s32[]{:S(2)}) async-start(), calls=%async_computation.9 | async-start | bytes 2359296 | tf_op jit(solution)/shard_map/all_gather | solution.py:16
  9.0 66.0 %copy-start = (f32[1024,128]{1,0:T(8,128)S(1)}, f32[1024,128]{1,0:T(8,128)}, u32[]{:S(2)}) copy-start(f32[1024,128]{1,0:T(8,128)} %param.5) | copy-start | bytes 1572868
  9.0 63.0 %reduce-scatter.10.cloned.1.call-start = ((), (), s32[]{:S(2)}) async-start(), calls=%async_computation.10 | async-start | bytes 1572864 | tf_op jit(solution)/shard_map/reduce_scatter | solution.py:18
  53.5 54.7 %all-gather.12.cloned.1.call-start = ((), (), s32[]{:S(2)}) async-start(), calls=%async_computation.11 | async-start | bytes 2359296 | tf_op jit(solution)/shard_map/all_gather | solution.py:16
  72.0 3.0 collective-permute-start
  75.9 67.3 %reduce-scatter.12.cloned.1.call-start = ((), (), s32[]{:S(2)}) async-start(), calls=%async_computation.12 | async-start | bytes 1572864 | tf_op jit(solution)/shard_map/reduce_scatter | solution.py:18
  124.6 54.8 %all-gather.14.cloned.1.call-start = ((), (), s32[]{:S(2)}) async-start(), calls=%async_computation.13 | async-start | bytes 2359296 | tf_op jit(solution)/shard_map/all_gather | solution.py:16
  143.2 1.7 collective-permute-start.1
  145.8 68.6 %reduce-scatter.14.cloned.1.call-start = ((), (), s32[]{:S(2)}) async-start(), calls=%async_computation.14 | async-start | bytes 1572864 | tf_op jit(solution)/shard_map/reduce_scatter | solution.py:18
  195.9 54.8 %all-gather.16.cloned.1.call-start = ((), (), s32[]{:S(2)}) async-start(), calls=%async_computation.15 | async-start | bytes 2359296 | tf_op jit(solution)/shard_map/all_gather | solution.py:16
  214.4 1.7 collective-permute-start.2
  217.0 68.6 %reduce-scatter.16.cloned.1.call-start = ((), (), s32[]{:S(2)}) async-start(), calls=%async_computation.16 | async-start | bytes 1572864 | tf_op jit(solution)/shard_map/reduce_scatter | solution.py:18
  267.1 54.7 %all-gather.18.cloned.1.call-start = ((), (), s32[]{:S(2)}) async-start(), calls=%async_computation.17 | async-start | bytes 2359296 | tf_op jit(solution)/shard_map/all_gather | solution.py:16
  285.7 1.7 collective-permute-start.3
  288.2 68.6 %reduce-scatter.18.cloned.1.call-start = ((), (), s32[]{:S(2)}) async-start(), calls=%async_computation.18 | async-start | bytes 1572864 | tf_op jit(solution)/shard_map/reduce_scatter | solution.py:18
  338.3 54.7 %all-gather.20.cloned.1.call-start = ((), (), s32[]{:S(2)}) async-start(), calls=%async_computation.19 | async-start | bytes 2359296 | tf_op jit(solution)/shard_map/all_gather | solution.py:16
  356.8 1.7 collective-permute-start.4
  359.4 68.6 %reduce-scatter.20.cloned.1.call-start = ((), (), s32[]{:S(2)}) async-start(), calls=%async_computation.20 | async-start | bytes 1572864 | tf_op jit(solution)/shard_map/reduce_scatter | solution.py:18
  409.5 54.7 %all-gather.22.cloned.1.call-start = ((), (), s32[]{:S(2)}) async-start(), calls=%async_computation.21 | async-start | bytes 2359296 | tf_op jit(solution)/shard_map/all_gather | solution.py:16
  428.0 1.7 collective-permute-start.5
  430.6 68.6 %reduce-scatter.22.cloned.1.call-start = ((), (), s32[]{:S(2)}) async-start(), calls=%async_computation.22 | async-start | bytes 1572864 | tf_op jit(solution)/shard_map/reduce_scatter | solution.py:18
  480.6 54.7 %all-gather.24.cloned.1.call-start = ((), (), s32[]{:S(2)}) async-start(), calls=%async_computation.23 | async-start | bytes 2359296 | tf_op jit(solution)/shard_map/all_gather | solution.py:16
  499.2 1.7 collective-permute-start.6
  501.7 68.6 %reduce-scatter.24.cloned.1.call-start = ((), (), s32[]{:S(2)}) async-start(), calls=%async_computation.24 | async-start | bytes 1572864 | tf_op jit(solution)/shard_map/reduce_scatter | solution.py:18
  551.8 55.0 %all-gather.26.cloned.1.call-start = ((), (), s32[]{:S(2)}) async-start(), calls=%async_computation.25 | async-start | bytes 2359296 | tf_op jit(solution)/shard_map/all_gather | solution.py:16
  570.4 1.7 collective-permute-start.7
  573.2 71.4 %copy-start.1 = (bf16[1024,128]{1,0:T(8,128)(2,1)S(1)}, bf16[1024,128]{1,0:T(8,128)(2,1)}, u32[]{:S(2)}) copy-start(bf16[1024,128]{1,0:T(8,128)(2,1)} %get-tuple-element.2) | copy-start | bytes 786436
  573.2 69.7 %reduce-scatter.26.cloned.1.call-start = ((), (), s32[]{:S(2)}) async-start(), calls=%async_computation.26 | async-start | bytes 1572864 | tf_op jit(solution)/shard_map/reduce_scatter | solution.py:18
  624.3 95.9 %all-reduce.2.cloned.1.call-start = ((), (), s32[]{:S(2)}) async-start(), calls=%async_computation.27 | async-start | bytes 131072 | tf_op jit(solution)/shard_map/psum | solution.py:31
  642.9 1.7 collective-permute-start.8
Sparse Core Ops, SparseCore 0:
  10.4 26.5 all-gather.9
  53.6 18.4 reduce-scatter.9
  76.0 32.1 all-gather.11
  124.7 18.4 reduce-scatter.11
  145.9 33.4 all-gather.13
  196.0 18.4 reduce-scatter.13
  217.1 33.4 all-gather.15
  267.2 18.4 reduce-scatter.15
  288.3 33.4 all-gather.17
  338.4 18.4 reduce-scatter.17
  359.5 33.4 all-gather.19
  409.6 18.4 reduce-scatter.19
  430.7 33.4 all-gather.21
  480.8 18.4 reduce-scatter.21
  501.9 33.4 all-gather.23
  551.9 18.4 reduce-scatter.23
  573.3 33.4 all-gather.25
  624.5 18.4 reduce-scatter.25
  647.7 72.5 all-reduce.1
where the time goes:
time: 729 us; the launch traced here: 728 us
  waiting for transfers between devices  536 us (74%)
  matrix products  150 us (21%)
  starting transfers between devices  16.4 us (2%)
  between operations  15.4 us (2%)
  other arithmetic  10.1 us (1%)
    all_gather x9, waiting for transfers between devices, apply_matrix(): src_block = lax.all_gather(y_low, 'row', axis=0, tiled=True)  295 us
    reduce_scatter x9, waiting for transfers between devices, apply_matrix(): folded = lax.psum_scatter(part_sum, 'col', scatter_dimension=0, tiled=True)  167 us
    dot_general x9, matrix products, apply_matrix(): part_sum = jnp.dot(mat_tile, src_block, preferred_element_type=jnp.float32)  149 us
    psum x1, waiting for transfers between devices, local_filter(): gram_mat = lax.psum(local_gram, both_axes) / (mat_tile.shape[0] * row_count)  74.8 us
    ppermute x9, starting transfers between devices, apply_matrix(): return lax.ppermute(folded, both_axes, realign_pairs)  15.2 us
  transfers between devices with their start and end apart: 28, of which 19 were waited for; matrix products, arithmetic and copies ran while one was open for 0% of the time, Pallas kernels for 0%

commit v1 on v0

v1 whole, which is shorter than its diff:
```python
import jax
import jax.numpy as jnp
from jax import lax
from jax.experimental import pallas as pl
from jax.experimental.pallas import tpu as pltpu
from jax.sharding import PartitionSpec as P

DEGREE = 8
W = 128
CH = 128
NC = 8
NM = 8
ROWS = 2048
COLS = 8192
PAN = 128
NPAN = ROWS // PAN
NST = 4
RB = 256
NT = (((1,), (1,)), ((), ()))
MESH = pl.DeviceIdType.MESH


def kernel(a_hbm, y_in, cen_ref, wid_ref, y_out, g_out,
           at, st, yg, part, xbuf, ycur, yprev, ysend, ystage, gacc, gbuf,
           a_sem, gr, gs, xr, xs, ss, y0r, y0s, yor, yos, rr, rs, ar, as_):
    i = lax.axis_index("row")
    z = lax.axis_index("col")
    c = lax.rem(i, 2)
    x = lax.rem(i // 2, 2)
    y = i // 4
    oc, ox, oy, oz = 1 - c, 1 - x, 1 - y, 1 - z
    flat = z * 8 + i
    aligned = y == z
    crossed = y != z

    def dev(xx, yy, zz, cc):
        return (zz, yy * 4 + xx * 2 + cc)

    plane = [dev(ox, y, z, c), dev(x, oy, z, c), dev(ox, oy, z, c)]
    twin = dev(x, y, z, oc)

    def slot(xx, yy, cc):
        return (xx * 2 + cc) * 2 + yy

    def slot0(xx, yy, cc):
        return yy * 4 + xx * 2 + cc

    def sources(fn):
        mine = fn(x, y, c)
        direct = [fn(ox, y, c), fn(x, oy, c), fn(ox, oy, c)]
        relayed = [fn(xx, yy, oc) for xx in (x, ox) for yy in (y, oy)]
        return mine, direct, relayed

    def load(p):
        return pltpu.make_async_copy(a_hbm.at[pl.ds(p * PAN, PAN), :], st.at[p % NST], a_sem.at[p % NST])

    def rcopy(src, dst, ssem, rsem, device):
        return pltpu.make_async_remote_copy(src_ref=src, dst_ref=dst, send_sem=ssem, recv_sem=rsem,
                                            device_id=device, device_id_type=MESH)

    def push(par, m, k, device):
        ref = yg.at[par, m, k]
        rcopy(ref, ref, gs.at[par], gr.at[par, m, k], device).start()

    def arrived(par, m, k):
        ref = yg.at[par, m, k]
        rcopy(ref, ref, gs.at[par], gr.at[par, m, k], twin).wait_recv()

    def distribute(par, m, k):
        for d in plane:
            push(par, m, k, d)
        push(par, m, k, twin)

    def sent(par):
        pltpu.make_async_copy(yg.at[par, pl.ds(0, 7)], yg.at[par, pl.ds(0, 7)], gs.at[par]).wait()

    for p in range(NST - 1):
        load(p).start()

    barrier = pltpu.get_barrier_semaphore()
    for d in range(1, 16):
        t = lax.rem(flat + d, 16)
        pl.semaphore_signal(barrier, inc=1, device_id=(t // 8, lax.rem(t, 8)), device_id_type=MESH)
    pl.semaphore_wait(barrier, 15)

    mine0, direct0, relayed0 = sources(slot0)
    for k in range(NC):
        t32 = y_in[k * CH:(k + 1) * CH, :].T
        ystage[k] = t32
        yg[0, mine0, k] = t32.astype(jnp.bfloat16)
        distribute(0, mine0, k)
    home = (lax.rem(flat, 2), flat // 2)
    stays = (home[0] == z) & (home[1] == i)
    y0_copy = rcopy(ystage, ycur, y0s, y0r, home)

    @pl.when(stays)
    def _():
        ycur[...] = ystage[...]

    @pl.when(jnp.logical_not(stays))
    def _():
        y0_copy.start()
    yprev[...] = jnp.zeros_like(yprev)

    for p in range(NPAN):
        if p + NST - 1 < NPAN:
            load(p + NST - 1).start()
        load(p).wait()
        for q in range(8):
            at[q * 1024:(q + 1) * 1024, p * PAN:(p + 1) * PAN] = st[p % NST, :, q * 1024:(q + 1) * 1024].T
        k = p - (NPAN - NC)
        if k >= 0:
            for m in direct0:
                arrived(0, m, k)
                push(0, m, k, twin)
    for k in range(NC):
        for m in relayed0:
            arrived(0, m, k)

    def xsend(par, k):
        return rcopy(part.at[par, oz, k], xbuf.at[par, k], xs.at[par], xr.at[par, k], dev(x, y, oz, c))

    def xsent(par):
        pltpu.make_async_copy(part.at[par, 0], part.at[par, 0], xs.at[par]).wait()

    def granule(par, cc, first, last):
        lhs = jnp.concatenate([yg[par, m, cc] for m in range(NM)], axis=1)
        for half in range(2):
            h = oz if half == 0 else z
            for q in range(1024 // RB):
                lanes = pl.ds(pl.multiple_of(h * 1024 + q * RB, RB), RB)
                rhs = jnp.concatenate([at[m * 1024 + cc * CH:m * 1024 + (cc + 1) * CH, lanes] for m in range(NM)], axis=0)
                res = jnp.dot(lhs, rhs, preferred_element_type=jnp.float32)
                for s in range(RB // CH):
                    k = q * (RB // CH) + s
                    val = res[:, s * CH:(s + 1) * CH]
                    if first:
                        part[par, h, k] = val
                    else:
                        part[par, h, k] = part[par, h, k] + val
                    if last and half == 0:
                        xsend(par, k).start()

    for cc in range(NC):
        granule(0, cc, cc == 0, cc == NC - 1)

    @pl.when(jnp.logical_not(stays))
    def _():
        y0_copy.wait()

    mine, direct, relayed = sources(slot)
    swap_to = dev(x, oy, oz, c)
    swap_slot = slot(x, oy, c)

    def summed(par, k):
        rcopy(part.at[par, oz, k], xbuf.at[par, k], xs.at[par], xr.at[par, k], dev(x, y, oz, c)).wait_recv()
        return part[par, z, k] + xbuf[par, k]

    def body(t, carry):
        par = lax.rem(t, 2)
        nxt = 1 - par
        center = cen_ref[0]
        width = wid_ref[0]
        scale = jnp.where(t == 0, 1.0, 2.0).astype(jnp.float32)
        keep = jnp.where(t == 0, 0.0, 1.0).astype(jnp.float32)

        def advance(k):
            total = summed(par, k)
            old = ycur[k]
            new = scale * (total - center * old) / width - keep * yprev[k]
            yprev[k] = old
            ycur[k] = new
            low = new.astype(jnp.bfloat16)

            @pl.when(aligned)
            def _():
                yg[nxt, mine, k] = low
                distribute(nxt, mine, k)

            @pl.when(crossed)
            def _():
                ysend[nxt, k] = low
                rcopy(ysend.at[nxt, k], yg.at[nxt, swap_slot, k], ss.at[nxt], gr.at[nxt, swap_slot, k], swap_to).start()

        def spread(k):
            @pl.when(crossed)
            def _():
                arrived(nxt, mine, k)
                distribute(nxt, mine, k)

        def relay(k):
            for m in direct:
                arrived(nxt, m, k)
                push(nxt, m, k, twin)

        sent(par)
        for step in range(NC + 3):
            if step < NC:
                advance(step)
            if 0 <= step - 1 < NC:
                spread(step - 1)
            if 0 <= step - 2 < NC:
                relay(step - 2)
            if 0 <= step - 3 < NC:
                k = step - 3
                for m in relayed:
                    arrived(nxt, m, k)
                granule(nxt, k, k == 0, k == NC - 1)
        xsent(par)

        @pl.when(crossed)
        def _():
            pltpu.make_async_copy(ysend.at[nxt], ysend.at[nxt], ss.at[nxt]).wait()
        return carry

    lax.fori_loop(0, DEGREE, body, 0)
    last = DEGREE % 2

    q = i * 2 + z
    place = (q // 8, lax.rem(q, 8))
    ends_here = (place[0] == z) & (place[1] == i)
    for k in range(NC):
        ystage_rows = ycur[k].T
        ystage[k] = ystage_rows
    out_copy = rcopy(ystage, y_out, yos, yor, place)

    @pl.when(ends_here)
    def _():
        y_out[...] = ystage[...]

    @pl.when(jnp.logical_not(ends_here))
    def _():
        out_copy.start()

    for k in range(NC):
        image = summed(last, k).astype(jnp.bfloat16)
        term = lax.dot_general(ycur[k].astype(jnp.bfloat16), image, NT, preferred_element_type=jnp.float32)
        if k == 0:
            gacc[...] = term
        else:
            gacc[...] += term
    xsent(last)
    sent(last)

    def ring(d):
        t = lax.rem(flat + d, 16)
        return t, (t // 8, lax.rem(t, 8))

    def rs_copy(d):
        t, device = ring(d)
        return rcopy(gacc.at[pl.ds(pl.multiple_of(t * 8, 8), 8), :], gbuf.at[d], rs.at[d], rr.at[d], device)

    for d in range(1, 16):
        rs_copy(d).start()
    own = pl.ds(pl.multiple_of(flat * 8, 8), 8)
    total = gacc[own, :]
    for d in range(1, 16):
        rs_copy(d).wait_recv()
        total = total + gbuf[d]
    g_out[own, :] = total * (1.0 / 16384)

    def ag_copy(d):
        return rcopy(g_out.at[own, :], g_out.at[own, :], as_.at[d], ar.at[d], ring(d)[1])

    for d in range(1, 16):
        ag_copy(d).start()
    for d in range(1, 16):
        ag_copy(d).wait()
        rs_copy(d).wait_send()

    @pl.when(jnp.logical_not(ends_here))
    def _():
        out_copy.wait()


def solution(mesh):
    both = ("col", "row")
    f32, bf16 = jnp.float32, jnp.bfloat16
    dma = pltpu.SemaphoreType.DMA
    vmem = pl.BlockSpec(memory_space=pltpu.VMEM)
    smem = pl.BlockSpec(memory_space=pltpu.SMEM)

    def local(mat_tile, y_start, center, half_width):
        y, g = pl.pallas_call(
            kernel,
            out_shape=(jax.ShapeDtypeStruct((NC, CH, W), f32), jax.ShapeDtypeStruct((W, W), f32)),
            in_specs=[pl.BlockSpec(memory_space=pl.ANY), vmem, smem, smem],
            out_specs=(vmem, vmem),
            scratch_shapes=[
                pltpu.VMEM((COLS, ROWS), bf16),
                pltpu.VMEM((NST, PAN, COLS), bf16),
                pltpu.VMEM((2, NM, NC, W, CH), bf16),
                pltpu.VMEM((2, 2, NC, W, CH), f32),
                pltpu.VMEM((2, NC, W, CH), f32),
                pltpu.VMEM((NC, W, CH), f32),
                pltpu.VMEM((NC, W, CH), f32),
                pltpu.VMEM((2, NC, W, CH), bf16),
                pltpu.VMEM((NC, W, CH), f32),
                pltpu.VMEM((W, W), f32),
                pltpu.VMEM((16, 8, W), f32),
                dma((NST,)),
                dma((2, NM, NC)),
                dma((2,)),
                dma((2, NC)),
                dma((2,)),
                dma((2,)),
                dma, dma, dma, dma,
                dma((16,)), dma((16,)), dma((16,)), dma((16,)),
            ],
            compiler_params=pltpu.CompilerParams(collective_id=0, has_side_effects=True, vmem_limit_bytes=67043328),
            name="chebyshev",
        )(mat_tile, y_start, center.reshape(1), half_width.reshape(1))
        return y.reshape(NC * CH, W), g

    return jax.shard_map(local, mesh=mesh, in_specs=(P("row", "col"), P(both, None), P(), P()),
                         out_specs=(P(both, None), P()), check_vma=False)
```

time: 729 us -> 311 us (0.43)
  waiting for transfers between devices: 536 us -> 0 us
  Pallas kernels: 0 us -> 306 us
  matrix products: 150 us -> 0 us
  starting transfers between devices: 16.4 us -> 0 us
  between operations: 15.4 us -> 1.93 us
  other arithmetic: 10.1 us -> 0 us
    pallas_call x0 -> x1, Pallas kernels: none -> 306 us  [local(): pl.pallas_call(kernel, out_shape=(jax.ShapeDtypeStruct((NC, CH, W), f32),...]
    all_gather x9 -> x0, waiting for transfers between devices: 295 us -> none  [apply_matrix(): src_block = lax.all_gather(y_low, 'row', axis=0, tiled=True)]
    reduce_scatter x9 -> x0, waiting for transfers between devices: 167 us -> none  [apply_matrix(): folded = lax.psum_scatter(part_sum, 'col', scatter_dimension=0, tiled=True)]
    dot_general x10 -> x0, matrix products: 150 us -> none  [the longest x9 149 us: apply_matrix(): part_sum = jnp.dot(mat_tile, src_block, preferred_element_type=jnp.float32)]
    psum x1 -> x0, waiting for transfers between devices: 74.8 us -> none  [local_filter(): gram_mat = lax.psum(local_gram, both_axes) / (mat_tile.shape[0] * row_count)]
    ppermute x9 -> x0, starting transfers between devices: 15.2 us -> none  [apply_matrix(): return lax.ppermute(folded, both_axes, realign_pairs)]
    convert_element_type x9 -> x0, other arithmetic: 8.67 us -> none  [the longest x7 5.79 us: local_filter(): y_cur.astype(jnp.bfloat16)]
  transfers between devices with their start and end apart: 28 -> 0, of which waited for: 19 -> 0; matrix products, arithmetic and copies ran while one was open for 0% -> 0% of each run, Pallas kernels for 0% -> 0%
where the time goes in v1:
time: 311 us
  Pallas kernels  306 us (98%)
  local copies, waits for them, and re-layouts  3.34 us (1%)
    pallas_call x1, Pallas kernels, local(): pl.pallas_call(kernel, out_shape=(jax.ShapeDtypeStruct((NC, CH, W), f32),...  306 us

profile of v1, /device:TPU:0, one launch (start us, length us, event | category | flops | bytes accessed | tf_op | source)
XLA Modules:
  0.0 311.0 jit_solution(10611581101282650288)
XLA Ops:
  1.9 305.7 %chebyshev.1 = (f32[8,128,128]{2,1,0:T(8,128)}, f32[128,128]{1,0:T(8,128)}) custom-call(bf16[2048,8192]{1,0:T(8,128)(2,1)} %a_hbm.1, f32[1024,128]{1,0:T(8,128)} %y_in.1, f32[1]{0:T(128)} %bitcast.3.cen_ref, f32[1]{0:T(128)} %bitcast.4.wid_ref), custom_call_target="tpu_custom_call" | custom-call | tf_op jit(solution)/shard_map/chebyshev/pallas_call | solution.py:284
  307.6 1.9 copy.10
  309.5 1.5 copy.11
